TPU v7x, 512 devices: a whole 4x8x8 slice. The times are simulated.
512 devices in a mesh: gx: 8 (over z), gy: 64 (over x, y, core).
Axes of the slice: x: 4, y: 8, z: 8, core: 2. Of those that a mesh axis runs over, the one named last changes fastest.
Arguments:
- right_side: float32 [4194304], P(('gx', 'gy')), may hold values from -60 to 60
- reaction: float32 [4194304], P(('gx', 'gy')), may hold values from 0.5 to 2
- cell_slots: int32 [125, 65536], P(None, ('gx', 'gy')), may hold values from 0 to 12543
- cell_level: int32 [65536], P(('gx', 'gy')), may hold values from 0 to 2
- con_masters: int32 [5, 131072], P(None, ('gx', 'gy')), may hold values from 0 to 12287
- con_rows: int32 [131072], P(('gx', 'gy')), may hold values from 0 to 9
- send_lists: int32 [8, 262144], P(None, ('gx', 'gy')), may hold values from 0 to 8191
Outputs:
- solution: float32 [4194304], P(('gx', 'gy'))
- residual: float32 [4194304], P(('gx', 'gy'))
Inputs may be any that keep to these rules, and one draw needn't show every extreme that they name: `cell_slots`: column block of rank d indexes d's local list: its 8192 owned unknowns, then 512 values from each of ranks d - 1, ..., d - 4, then from d + 1, ..., d + 4, then its 256 constrained values (rank d = 64 gx + gy). `cell_level`: A cell of level l has side 2^(-l). `con_masters`: slots among the same rank's owned and ghost values. `con_rows`: row of the interpolation table: 5 fine nodes on each half of a coarse edge. `send_lists`: row j of rank s lists s's owned unknowns that fill ghost block j of rank s + j + 1 (j < 4) or of rank s - (j - 3); rows without such a rank are unused.
All inputs are finite; a program needn't handle non-finite values.
Results may differ from a plain program's by a relative error of at most 0.0002.
Values sent between devices are 32-bit elements; how exact they have to be, the bound alone decides.
No kernel may reach another device: no remote copies, remote signals or barrier semaphores. Data moves between devices by JAX's collectives and lax.ppermute only.
A program may use at most 64 MiB of HBM per device.

v0:
```python
import jax
import jax.numpy as jnp
import numpy as np
from jax import lax
from jax.sharding import Mesh
from jax.sharding import PartitionSpec as P

ITERS = 3
GX_GY = ("gx", "gy_0", "gy_1", "gy_2")


def shifted(value, axis, steps):
    count = lax.axis_size(axis)
    initial, last = (max(0, -steps), min(count, count - steps))
    return lax.ppermute(value, axis, [(source, source + steps) for source in range(initial, last)])


def one_axis_at_a_time(x, axes):
    for axis in axes:
        x = lax.psum(x, axis)
    return x


def lagrange(node_list, points):
    node_count = len(node_list)
    values = np.ones((len(points), node_count))
    derivs = np.zeros((len(points), node_count))
    for basis_node in range(node_count):
        for other_node in range(node_count):
            if other_node != basis_node:
                values[:, basis_node] = (
                    values[:, basis_node]
                    * (points - node_list[other_node])
                    / (node_list[basis_node] - node_list[other_node])
                )
        for skipped in range(node_count):
            if skipped != basis_node:
                product_term = np.ones(len(points)) / (node_list[basis_node] - node_list[skipped])
                for other_node in range(node_count):
                    if other_node != basis_node and other_node != skipped:
                        product_term = (
                            product_term
                            * (points - node_list[other_node])
                            / (node_list[basis_node] - node_list[other_node])
                        )
                derivs[:, basis_node] = derivs[:, basis_node] + product_term
    return (values, derivs)


def tables():
    gll_offset = np.sqrt(3.0 / 7.0)
    lobatto = np.array([0.0, (1.0 - gll_offset) / 2.0, 0.5, (1.0 + gll_offset) / 2.0, 1.0])
    inner_point = np.sqrt(5.0 - 2.0 * np.sqrt(10.0 / 7.0)) / 3.0
    outer_point = np.sqrt(5.0 + 2.0 * np.sqrt(10.0 / 7.0)) / 3.0
    inner_weight = (322.0 + 13.0 * np.sqrt(70.0)) / 900.0
    outer_weight = (322.0 - 13.0 * np.sqrt(70.0)) / 900.0
    points = np.array([-outer_point, -inner_point, 0.0, inner_point, outer_point])
    gauss_weights = np.array(
        [outer_weight, inner_weight, 128.0 / 225.0, inner_weight, outer_weight]
    )
    points = (points + 1.0) / 2.0
    gauss_weights = gauss_weights / 2.0
    shapes, slopes = lagrange(lobatto, points)
    fine_points = np.concatenate([lobatto / 2.0, (1.0 + lobatto) / 2.0])
    interp, unused_slopes = lagrange(lobatto, fine_points)
    quad_weights = np.kron(gauss_weights, np.kron(gauss_weights, gauss_weights))
    grad_x = np.kron(slopes, np.kron(shapes, shapes))
    grad_y = np.kron(shapes, np.kron(slopes, shapes))
    grad_z = np.kron(shapes, np.kron(shapes, slopes))
    stiffness = np.zeros((125, 125))
    for gradient in (grad_x, grad_y, grad_z):
        stiffness = stiffness + gradient.T @ (quad_weights[:, None] * gradient)
    return (jnp.asarray(interp, jnp.float32), jnp.asarray(stiffness, jnp.float32))


def cell_laplace(cell_values, cell_scale, stiffness):
    product = jnp.dot(
        stiffness, cell_values, precision=lax.Precision.HIGHEST, preferred_element_type=jnp.float32
    )
    return product * cell_scale[None, :]


def local_apply(own_values, ghosts, slot_map, cell_scale, masters, weights, stiffness):
    local_list = jnp.concatenate([own_values, ghosts.reshape(-1)])
    picked = local_list[masters]
    resolved = jnp.sum(weights * picked, axis=0)
    full_list = jnp.concatenate([local_list, resolved])
    cell_values = full_list[slot_map]
    contrib = cell_laplace(cell_values, cell_scale, stiffness)
    summed = (
        jnp.zeros(full_list.shape, jnp.float32).at[slot_map.reshape(-1)].add(contrib.reshape(-1))
    )
    split_at = local_list.shape[0]
    spread = (
        summed[:split_at]
        .at[masters.reshape(-1)]
        .add((weights * summed[split_at:][None, :]).reshape(-1))
    )
    return spread


def on_device(right_side, reaction, cell_slots, cell_level, con_masters, con_rows, send_lists):
    interp, stiffness = tables()
    block_count = send_lists.shape[0]
    half_count = block_count // 2
    offsets = [neighbour + 1 for neighbour in range(half_count)] + [
        -(neighbour + 1) for neighbour in range(half_count)
    ]
    cell_scale = jnp.exp2(-cell_level.astype(jnp.float32))
    selector = (con_rows[None, :] == jnp.arange(10, dtype=jnp.int32)[:, None]).astype(jnp.float32)
    weights = jnp.dot(interp.T, selector, precision=lax.Precision.HIGHEST)
    own_count = right_side.shape[0]
    flat_lists = send_lists.reshape(-1)

    def carry_out(packed):
        return jnp.stack(
            [
                shifted(packed[neighbour], GX_GY, offsets[neighbour])
                for neighbour in range(block_count)
            ]
        )

    def carry_back(packed):
        return jnp.stack(
            [
                shifted(packed[neighbour], GX_GY, -offsets[neighbour])
                for neighbour in range(block_count)
            ]
        )

    def operate(vector):
        ghosts = carry_out(vector[send_lists])
        spread = local_apply(
            vector, ghosts, cell_slots, cell_scale, con_masters, weights, stiffness
        )
        returned = carry_back(spread[own_count:].reshape(block_count, -1))
        result = spread[:own_count] + reaction * vector
        return result.at[flat_lists].add(returned.reshape(-1))

    def paired_sums(vector, applied):
        return (
            one_axis_at_a_time(jnp.sum(vector * vector), GX_GY),
            one_axis_at_a_time(jnp.sum(vector * applied), GX_GY),
        )

    solution = jnp.zeros_like(right_side)
    residual = right_side
    applied = operate(residual)
    norm_now, product = paired_sums(residual, applied)
    step_size = norm_now / product
    direction = residual
    applied_dir = applied
    for iteration in range(ITERS):
        solution = solution + step_size * direction
        residual = residual - step_size * applied_dir
        if iteration + 1 < ITERS:
            applied = operate(residual)
            norm_next, product = paired_sums(residual, applied)
            beta_ratio = norm_next / norm_now
            step_size = norm_next / (product - beta_ratio * norm_next / step_size)
            direction = residual + beta_ratio * direction
            applied_dir = applied + beta_ratio * applied_dir
            norm_now = norm_next
    return (solution, residual)


def solution(mesh):
    torus = Mesh(mesh.devices.reshape(mesh.shape["gx"], 4, 8, 2), ("gx", "gy_0", "gy_1", "gy_2"))
    placed = (
        P(GX_GY),
        P(GX_GY),
        P(None, GX_GY),
        P(GX_GY),
        P(None, GX_GY),
        P(GX_GY),
        P(None, GX_GY),
    )
    return jax.shard_map(
        on_device, mesh=torus, in_specs=placed, out_specs=(P(GX_GY), P(GX_GY)), check_vma=False
    )
```

profile of v0, /device:TPU:1, one launch (start us, length us, event | category | flops | bytes accessed | tf_op | source)
XLA Modules:
  0.0 1038.3 jit_solution(5382295155196519492)
XLA Ops:
  2.1 23.0 %gather_fusion = f32[4096]{0:T(1024)S(1)} fusion(f32[8192]{0:T(1024)S(1)} %copy-done, s32[4096]{0:T(1024)S(1)} %broadcast_clamp_fusion), kind=kCustom, calls=%fused_computation | custom fusion | bytes 49152 | tf_op jit(solution)/shard_map/gather | solution.py:132
  29.1 8.7 collective-permute-start.4
  65.4 82.3 %gather_fusion.2 = f32[16000]{0:T(1024)S(1)} fusion(f32[12544]{0:T(1024)S(1)} %pad_maximum_fusion, s32[16384]{0:T(1024)S(1)} %pad_clamp_fusion), kind=kCustom, calls=%fused_computation.2 | custom fusion | bytes 192000 | tf_op jit(solution)/shard_map/gather | solution.py:88
  148.1 85.1 %scatter_custom_fusion = f32[12544]{0:T(1024)S(1)} fusion(s32[16000]{0:T(1024)S(1)} %fusion.7, f32[16000]{0:T(1024)S(1)} %bitcast.115, f32[]{:T(128)} %constant.8.clone.1), kind=kCustom, calls=%fused_computation.59 | custom fusion | flops 16000 | bytes 50180 | tf_op jit(solution)/shard_map/scatter-add | solution.py:91
  233.3 7.4 scatter_fusion
  261.9 22.5 %scatter_fusion.1 = f32[8192]{0:T(1024)S(1)} fusion(f32[8192]{0:T(1024)S(1)} %slice_add_fusion.2, s32[4096]{0:T(1024)S(1)} %bitcast.101, f32[4096]{0:T(1024)S(1)} %bitcast.112), kind=kCustom, calls=%fused_computation.11 | custom fusion | flops 4096 | bytes 65536 | tf_op jit(solution)/shard_map/scatter-add | solution.py:138
  285.0 32.7 %all-reduce.5 = (f32[]{:T(128)}, f32[]{:T(128)}) all-reduce(f32[]{:T(128)} %get-tuple-element.7, f32[]{:T(128)} %get-tuple-element.6), channel_id=1, replica_groups=mesh['gx'=8,'gy_0'=4,'gy_1'=8,'gy_2'=2] {'gx'}, use_global_device_ids=true, to_apply=%region_1.0 | all-reduce | flops 2 | bytes 16 | tf_op jit(solution)/shard_map/psum | solution.py:20
  324.2 16.9 %all-reduce.2 = (f32[]{:T(128)}, f32[]{:T(128)}) all-reduce(f32[]{:T(128)} %get-tuple-element.24, f32[]{:T(128)} %get-tuple-element.25), channel_id=1, replica_groups=mesh['gx'=8,'gy_0'=4,'gy_1'=8,'gy_2'=2] {'gy_1'}, use_global_device_ids=true, to_apply=%region_3.0 | all-reduce | flops 2 | bytes 16 | tf_op jit(solution)/shard_map/psum | solution.py:20
  341.1 10.0 all-reduce.11
  352.4 23.0 %gather_fusion.3 = f32[4096]{0:T(1024)S(1)} fusion(f32[8192]{0:T(1024)S(1)} %multiply_subtract_fusion.2, s32[4096]{0:T(1024)S(1)} %broadcast_clamp_fusion), kind=kCustom, calls=%fused_computation.3 | custom fusion | bytes 49152 | tf_op jit(solution)/shard_map/gather | solution.py:132
  408.0 82.3 %gather_fusion.5 = f32[16000]{0:T(1024)S(1)} fusion(f32[12544]{0:T(1024)S(1)} %pad_maximum_fusion.1, s32[16384]{0:T(1024)S(1)} %pad_clamp_fusion), kind=kCustom, calls=%fused_computation.5 | custom fusion | bytes 192000 | tf_op jit(solution)/shard_map/gather | solution.py:88
  490.7 85.1 %scatter_custom_fusion.3 = f32[12544]{0:T(1024)S(1)} fusion(s32[16000]{0:T(1024)S(1)} %fusion.7, f32[16000]{0:T(1024)S(1)} %bitcast.116, f32[]{:T(128)} %constant.8.clone.1), kind=kCustom, calls=%fused_computation.57 | custom fusion | flops 16000 | bytes 50180 | tf_op jit(solution)/shard_map/scatter-add | solution.py:91
  575.9 7.6 scatter_fusion.2
  605.4 22.5 %scatter_fusion.3 = f32[8192]{0:T(1024)S(1)} fusion(f32[8192]{0:T(1024)S(1)} %slice_add_fusion.1, s32[4096]{0:T(1024)S(1)} %bitcast.102, f32[4096]{0:T(1024)S(1)} %bitcast.113), kind=kCustom, calls=%fused_computation.14 | custom fusion | flops 4096 | bytes 65536 | tf_op jit(solution)/shard_map/scatter-add | solution.py:138
  628.6 25.6 %all-reduce.4 = (f32[]{:T(128)}, f32[]{:T(128)}) all-reduce(f32[]{:T(128)} %get-tuple-element.5, f32[]{:T(128)} %get-tuple-element.4), channel_id=1, replica_groups=mesh['gx'=8,'gy_0'=4,'gy_1'=8,'gy_2'=2] {'gx'}, use_global_device_ids=true, to_apply=%region_15.0 | all-reduce | flops 2 | bytes 16 | tf_op jit(solution)/shard_map/psum | solution.py:20
  660.9 20.6 %all-reduce.1 = (f32[]{:T(128)}, f32[]{:T(128)}) all-reduce(f32[]{:T(128)} %get-tuple-element.22, f32[]{:T(128)} %get-tuple-element.23), channel_id=1, replica_groups=mesh['gx'=8,'gy_0'=4,'gy_1'=8,'gy_2'=2] {'gy_1'}, use_global_device_ids=true, to_apply=%region_17.0 | all-reduce | flops 2 | bytes 16 | tf_op jit(solution)/shard_map/psum | solution.py:20
  681.5 9.6 all-reduce.10
  695.7 23.0 %gather_fusion.6 = f32[4096]{0:T(1024)S(1)} fusion(f32[8192]{0:T(1024)S(1)} %multiply_subtract_fusion.1, s32[4096]{0:T(1024)S(1)} %broadcast_clamp_fusion), kind=kCustom, calls=%fused_computation.6 | custom fusion | bytes 49152 | tf_op jit(solution)/shard_map/gather | solution.py:132
  751.2 82.3 %gather_fusion.8 = f32[16000]{0:T(1024)S(1)} fusion(f32[12544]{0:T(1024)S(1)} %pad_maximum_fusion.2, s32[16384]{0:T(1024)S(1)} %pad_clamp_fusion), kind=kCustom, calls=%fused_computation.8 | custom fusion | bytes 192000 | tf_op jit(solution)/shard_map/gather | solution.py:88
  833.9 85.1 %scatter_custom_fusion.6 = f32[12544]{0:T(1024)S(1)} fusion(s32[16000]{0:T(1024)S(1)} %fusion.7, f32[16000]{0:T(1024)S(1)} %bitcast.114, f32[]{:T(128)} %constant.8.clone.1), kind=kCustom, calls=%fused_computation.55 | custom fusion | flops 16000 | bytes 50180 | tf_op jit(solution)/shard_map/scatter-add | solution.py:91
  948.5 22.5 %scatter_fusion.5 = f32[8192]{0:T(1024)S(1)} fusion(f32[8192]{0:T(1024)S(1)} %slice_add_fusion, s32[4096]{0:T(1024)S(1)} %bitcast.103, f32[4096]{0:T(1024)S(1)} %bitcast.111), kind=kCustom, calls=%fused_computation.17 | custom fusion | flops 4096 | bytes 65536 | tf_op jit(solution)/shard_map/scatter-add | solution.py:138
  971.5 25.5 %all-reduce.3 = (f32[]{:T(128)}, f32[]{:T(128)}) all-reduce(f32[]{:T(128)} %get-tuple-element.3, f32[]{:T(128)} %get-tuple-element.2), channel_id=1, replica_groups=mesh['gx'=8,'gy_0'=4,'gy_1'=8,'gy_2'=2] {'gx'}, use_global_device_ids=true, to_apply=%region_29.0 | all-reduce | flops 2 | bytes 16 | tf_op jit(solution)/shard_map/psum | solution.py:20
  1003.7 20.0 %all-reduce = (f32[]{:T(128)}, f32[]{:T(128)}) all-reduce(f32[]{:T(128)} %get-tuple-element.20, f32[]{:T(128)} %get-tuple-element.21), channel_id=1, replica_groups=mesh['gx'=8,'gy_0'=4,'gy_1'=8,'gy_2'=2] {'gy_1'}, use_global_device_ids=true, to_apply=%region_31.0 | all-reduce | flops 2 | bytes 16 | tf_op jit(solution)/shard_map/psum | solution.py:20
  1023.6 10.1 all-reduce.9
  (191 shorter events, 193.0 us)
Async XLA Ops:
  25.2 19.5 %collective-permute-start.7 = (f32[512]{0:T(512)S(1)}, f32[512]{0:T(512)S(1)}, u32[]{:S(2)}, u32[]{:S(2)}) collective-permute-start(f32[512]{0:T(512)S(1)} %get-tuple-element.74), channel_id=1, source_target_pairs={{4,0},{5,1},{6,2},{7,3},{8,4},{9,5},{10,6},{11,7},{12,8},{13,9},{1... | collective-permute-start | bytes 6152 | tf_op jit(solution)/shard_map/ppermute | solution.py:15
  26.5 24.4 %collective-permute-start.6 = (f32[512]{0:T(512)S(1)}, f32[512]{0:T(512)S(1)}, u32[]{:S(2)}, u32[]{:S(2)}) collective-permute-start(f32[512]{0:T(512)S(1)} %get-tuple-element.75), channel_id=1, source_target_pairs={{3,0},{4,1},{5,2},{6,3},{7,4},{8,5},{9,6},{10,7},{11,8},{12,9},{13... | collective-permute-start | bytes 6152 | tf_op jit(solution)/shard_map/ppermute | solution.py:15
  27.8 26.5 %collective-permute-start.5 = (f32[512]{0:T(512)S(1)}, f32[512]{0:T(512)S(1)}, u32[]{:S(2)}, u32[]{:S(2)}) collective-permute-start(f32[512]{0:T(512)S(1)} %get-tuple-element.76), channel_id=1, source_target_pairs={{2,0},{3,1},{4,2},{5,3},{6,4},{7,5},{8,6},{9,7},{10,8},{11,9},{12,... | collective-permute-start | bytes 6152 | tf_op jit(solution)/shard_map/ppermute | solution.py:15
  29.1 27.1 %collective-permute-start.4 = (f32[512]{0:T(512)S(1)}, f32[512]{0:T(512)S(1)}, u32[]{:S(2)}, u32[]{:S(2)}) collective-permute-start(f32[512]{0:T(512)S(1)} %get-tuple-element.77), channel_id=1, source_target_pairs={{1,0},{2,1},{3,2},{4,3},{5,4},{6,5},{7,6},{8,7},{9,8},{10,9},{11,1... | collective-permute-start | bytes 6152 | tf_op jit(solution)/shard_map/ppermute | solution.py:15
  37.8 18.4 %collective-permute-start.3 = (f32[512]{0:T(512)S(1)}, f32[512]{0:T(512)S(1)}, u32[]{:S(2)}, u32[]{:S(2)}) collective-permute-start(f32[512]{0:T(512)S(1)} %get-tuple-element.78), channel_id=1, source_target_pairs={{0,4},{1,5},{2,6},{3,7},{4,8},{5,9},{6,10},{7,11},{8,12},{9,13},{1... | collective-permute-start | bytes 6152 | tf_op jit(solution)/shard_map/ppermute | solution.py:15
  44.6 11.6 %collective-permute-start.2 = (f32[512]{0:T(512)S(1)}, f32[512]{0:T(512)S(1)}, u32[]{:S(2)}, u32[]{:S(2)}) collective-permute-start(f32[512]{0:T(512)S(1)} %get-tuple-element.79), channel_id=1, source_target_pairs={{0,3},{1,4},{2,5},{3,6},{4,7},{5,8},{6,9},{7,10},{8,11},{9,12},{10... | collective-permute-start | bytes 6152 | tf_op jit(solution)/shard_map/ppermute | solution.py:15
  240.8 13.1 %collective-permute-start.15 = (f32[512]{0:T(512)S(1)}, f32[512]{0:T(512)S(1)}, u32[]{:S(2)}, u32[]{:S(2)}) collective-permute-start(f32[512]{0:T(512)S(1)} %get-tuple-element.48), channel_id=1, source_target_pairs={{0,4},{1,5},{2,6},{3,7},{4,8},{5,9},{6,10},{7,11},{8,12},{9,13},{1... | collective-permute-start | bytes 6152 | tf_op jit(solution)/shard_map/ppermute | solution.py:15
  242.6 12.6 %collective-permute-start.14 = (f32[512]{0:T(512)S(1)}, f32[512]{0:T(512)S(1)}, u32[]{:S(2)}, u32[]{:S(2)}) collective-permute-start(f32[512]{0:T(512)S(1)} %get-tuple-element.49), channel_id=1, source_target_pairs={{0,3},{1,4},{2,5},{3,6},{4,7},{5,8},{6,9},{7,10},{8,11},{9,12},{10... | collective-permute-start | bytes 6152 | tf_op jit(solution)/shard_map/ppermute | solution.py:15
  375.5 12.6 %collective-permute-start.23 = (f32[512]{0:T(512)S(1)}, f32[512]{0:T(512)S(1)}, u32[]{:S(2)}, u32[]{:S(2)}) collective-permute-start(f32[512]{0:T(512)S(1)} %get-tuple-element.66), channel_id=1, source_target_pairs={{4,0},{5,1},{6,2},{7,3},{8,4},{9,5},{10,6},{11,7},{12,8},{13,9},{1... | collective-permute-start | bytes 6152 | tf_op jit(solution)/shard_map/ppermute | solution.py:15
  376.8 17.5 %collective-permute-start.22 = (f32[512]{0:T(512)S(1)}, f32[512]{0:T(512)S(1)}, u32[]{:S(2)}, u32[]{:S(2)}) collective-permute-start(f32[512]{0:T(512)S(1)} %get-tuple-element.67), channel_id=1, source_target_pairs={{3,0},{4,1},{5,2},{6,3},{7,4},{8,5},{9,6},{10,7},{11,8},{12,9},{13... | collective-permute-start | bytes 6152 | tf_op jit(solution)/shard_map/ppermute | solution.py:15
  378.1 19.6 %collective-permute-start.21 = (f32[512]{0:T(512)S(1)}, f32[512]{0:T(512)S(1)}, u32[]{:S(2)}, u32[]{:S(2)}) collective-permute-start(f32[512]{0:T(512)S(1)} %get-tuple-element.68), channel_id=1, source_target_pairs={{2,0},{3,1},{4,2},{5,3},{6,4},{7,5},{8,6},{9,7},{10,8},{11,9},{12,... | collective-permute-start | bytes 6152 | tf_op jit(solution)/shard_map/ppermute | solution.py:15
  379.4 20.4 %collective-permute-start.20 = (f32[512]{0:T(512)S(1)}, f32[512]{0:T(512)S(1)}, u32[]{:S(2)}, u32[]{:S(2)}) collective-permute-start(f32[512]{0:T(512)S(1)} %get-tuple-element.69), channel_id=1, source_target_pairs={{1,0},{2,1},{3,2},{4,3},{5,4},{6,5},{7,6},{8,7},{9,8},{10,9},{11,1... | collective-permute-start | bytes 6152 | tf_op jit(solution)/shard_map/ppermute | solution.py:15
  381.7 18.1 %collective-permute-start.19 = (f32[512]{0:T(512)S(1)}, f32[512]{0:T(512)S(1)}, u32[]{:S(2)}, u32[]{:S(2)}) collective-permute-start(f32[512]{0:T(512)S(1)} %get-tuple-element.70), channel_id=1, source_target_pairs={{0,4},{1,5},{2,6},{3,7},{4,8},{5,9},{6,10},{7,11},{8,12},{9,13},{1... | collective-permute-start | bytes 6152 | tf_op jit(solution)/shard_map/ppermute | solution.py:15
  388.1 11.7 %collective-permute-start.18 = (f32[512]{0:T(512)S(1)}, f32[512]{0:T(512)S(1)}, u32[]{:S(2)}, u32[]{:S(2)}) collective-permute-start(f32[512]{0:T(512)S(1)} %get-tuple-element.71), channel_id=1, source_target_pairs={{0,3},{1,4},{2,5},{3,6},{4,7},{5,8},{6,9},{7,10},{8,11},{9,12},{10... | collective-permute-start | bytes 6152 | tf_op jit(solution)/shard_map/ppermute | solution.py:15
  583.5 13.8 %collective-permute-start.31 = (f32[512]{0:T(512)S(1)}, f32[512]{0:T(512)S(1)}, u32[]{:S(2)}, u32[]{:S(2)}) collective-permute-start(f32[512]{0:T(512)S(1)} %get-tuple-element.40), channel_id=1, source_target_pairs={{0,4},{1,5},{2,6},{3,7},{4,8},{5,9},{6,10},{7,11},{8,12},{9,13},{1... | collective-permute-start | bytes 6152 | tf_op jit(solution)/shard_map/ppermute | solution.py:15
  585.4 13.2 %collective-permute-start.30 = (f32[512]{0:T(512)S(1)}, f32[512]{0:T(512)S(1)}, u32[]{:S(2)}, u32[]{:S(2)}) collective-permute-start(f32[512]{0:T(512)S(1)} %get-tuple-element.41), channel_id=1, source_target_pairs={{0,3},{1,4},{2,5},{3,6},{4,7},{5,8},{6,9},{7,10},{8,11},{9,12},{10... | collective-permute-start | bytes 6152 | tf_op jit(solution)/shard_map/ppermute | solution.py:15
  718.7 12.6 %collective-permute-start.39 = (f32[512]{0:T(512)S(1)}, f32[512]{0:T(512)S(1)}, u32[]{:S(2)}, u32[]{:S(2)}) collective-permute-start(f32[512]{0:T(512)S(1)} %get-tuple-element.58), channel_id=1, source_target_pairs={{4,0},{5,1},{6,2},{7,3},{8,4},{9,5},{10,6},{11,7},{12,8},{13,9},{1... | collective-permute-start | bytes 6152 | tf_op jit(solution)/shard_map/ppermute | solution.py:15
  720.0 17.5 %collective-permute-start.38 = (f32[512]{0:T(512)S(1)}, f32[512]{0:T(512)S(1)}, u32[]{:S(2)}, u32[]{:S(2)}) collective-permute-start(f32[512]{0:T(512)S(1)} %get-tuple-element.59), channel_id=1, source_target_pairs={{3,0},{4,1},{5,2},{6,3},{7,4},{8,5},{9,6},{10,7},{11,8},{12,9},{13... | collective-permute-start | bytes 6152 | tf_op jit(solution)/shard_map/ppermute | solution.py:15
  721.3 19.6 %collective-permute-start.37 = (f32[512]{0:T(512)S(1)}, f32[512]{0:T(512)S(1)}, u32[]{:S(2)}, u32[]{:S(2)}) collective-permute-start(f32[512]{0:T(512)S(1)} %get-tuple-element.60), channel_id=1, source_target_pairs={{2,0},{3,1},{4,2},{5,3},{6,4},{7,5},{8,6},{9,7},{10,8},{11,9},{12,... | collective-permute-start | bytes 6152 | tf_op jit(solution)/shard_map/ppermute | solution.py:15
  722.6 20.4 %collective-permute-start.36 = (f32[512]{0:T(512)S(1)}, f32[512]{0:T(512)S(1)}, u32[]{:S(2)}, u32[]{:S(2)}) collective-permute-start(f32[512]{0:T(512)S(1)} %get-tuple-element.61), channel_id=1, source_target_pairs={{1,0},{2,1},{3,2},{4,3},{5,4},{6,5},{7,6},{8,7},{9,8},{10,9},{11,1... | collective-permute-start | bytes 6152 | tf_op jit(solution)/shard_map/ppermute | solution.py:15
  724.9 18.1 %collective-permute-start.35 = (f32[512]{0:T(512)S(1)}, f32[512]{0:T(512)S(1)}, u32[]{:S(2)}, u32[]{:S(2)}) collective-permute-start(f32[512]{0:T(512)S(1)} %get-tuple-element.62), channel_id=1, source_target_pairs={{0,4},{1,5},{2,6},{3,7},{4,8},{5,9},{6,10},{7,11},{8,12},{9,13},{1... | collective-permute-start | bytes 6152 | tf_op jit(solution)/shard_map/ppermute | solution.py:15
  731.3 11.7 %collective-permute-start.34 = (f32[512]{0:T(512)S(1)}, f32[512]{0:T(512)S(1)}, u32[]{:S(2)}, u32[]{:S(2)}) collective-permute-start(f32[512]{0:T(512)S(1)} %get-tuple-element.63), channel_id=1, source_target_pairs={{0,3},{1,4},{2,5},{3,6},{4,7},{5,8},{6,9},{7,10},{8,11},{9,12},{10... | collective-permute-start | bytes 6152 | tf_op jit(solution)/shard_map/ppermute | solution.py:15
  926.5 13.8 %collective-permute-start.47 = (f32[512]{0:T(512)S(1)}, f32[512]{0:T(512)S(1)}, u32[]{:S(2)}, u32[]{:S(2)}) collective-permute-start(f32[512]{0:T(512)S(1)} %get-tuple-element.32), channel_id=1, source_target_pairs={{0,4},{1,5},{2,6},{3,7},{4,8},{5,9},{6,10},{7,11},{8,12},{9,13},{1... | collective-permute-start | bytes 6152 | tf_op jit(solution)/shard_map/ppermute | solution.py:15
  928.4 13.2 %collective-permute-start.46 = (f32[512]{0:T(512)S(1)}, f32[512]{0:T(512)S(1)}, u32[]{:S(2)}, u32[]{:S(2)}) collective-permute-start(f32[512]{0:T(512)S(1)} %get-tuple-element.33), channel_id=1, source_target_pairs={{0,3},{1,4},{2,5},{3,6},{4,7},{5,8},{6,9},{7,10},{8,11},{9,12},{10... | collective-permute-start | bytes 6152 | tf_op jit(solution)/shard_map/ppermute | solution.py:15
  (33 other events, 361.1 us)
where the time goes:
time: 1040 us
  other arithmetic  349 us (34%)
  local copies, waits for them, and re-layouts  339 us (33%)
  blocking collectives  191 us (18%)
  starting transfers between devices  133 us (13%)
  waiting for transfers between devices  13.3 us (1%)
  between operations  11.8 us (1%)
    scatter-add x3, other arithmetic, local_apply(): jnp.zeros(full_list.shape, jnp.float32).at[slot_map.reshape(-1)]  255 us
    gather x3, local copies, waits for them, and re-layouts, local_apply(): cell_values = full_list[slot_map]  247 us
    psum x12, blocking collectives, one_axis_at_a_time(): x = lax.psum(x, axis)  191 us
    ppermute x48, starting transfers between devices, shifted(): lax.ppermute(value, axis, [(source, source + steps) for source in range(i...  133 us
    gather x3, local copies, waits for them, and re-layouts, operate(): ghosts = carry_out(vector[send_lists])  69.1 us
    scatter-add x3, other arithmetic, operate(): return result.at[flat_lists].add(returned.reshape(-1))  67.4 us
    scatter-add x3, other arithmetic, local_apply(): spread = summed[:split_at].at[masters.reshape(-1)].add((weights * summed[...  22.4 us
    gather x6, local copies, waits for them, and re-layouts, local_apply(): picked = local_list[masters]  21.3 us
  transfers between devices with their start and end apart: 48, of which 12 were waited for; matrix products, arithmetic and copies ran while one was open for 0% of the time, Pallas kernels for 0%

commit v1 on v0

--- a/solution.py
+++ b/solution.py
@@ -17,7 +17,7 @@
 
 def one_axis_at_a_time(x, axes):
     for axis in axes:
-        x = lax.psum(x, axis)
+        x = jnp.sum(lax.all_gather(x, axis_name=axis), axis=0)
     return x
 
 

time: 1040 us -> 1090 us (1.048)
  local copies, waits for them, and re-layouts: 339 us -> 378 us
  other arithmetic: 349 us -> 364 us
  blocking collectives: 191 us -> 178 us
    psum x12 -> x0, blocking collectives: 191 us -> none  [one_axis_at_a_time(): x = lax.psum(x, axis)]
    unnamed x0 -> x12, blocking collectives: none -> 178 us
    unnamed x27 -> x79, local copies, waits for them, and re-layouts: 1.53 us -> 40.2 us
    reduce_sum x0 -> x24, other arithmetic: none -> 14.8 us  [one_axis_at_a_time(): x = jnp.sum(lax.all_gather(x, axis_name=axis), axis=0)]
  transfers between devices with their start and end apart: 48 -> 48, of which waited for: 12 -> 10; matrix products, arithmetic and copies ran while one was open for 0% -> 0% of each run, Pallas kernels for 0% -> 0%
where the time goes in v1:
time: 1090 us
  local copies, waits for them, and re-layouts  378 us (35%)
  other arithmetic  364 us (33%)
  blocking collectives  178 us (16%)
  starting transfers between devices  141 us (13%)
  waiting for transfers between devices  12.6 us (1%)
  between operations  11.7 us (1%)
    scatter-add x3, other arithmetic, local_apply(): jnp.zeros(full_list.shape, jnp.float32).at[slot_map.reshape(-1)]  255 us
    gather x3, local copies, waits for them, and re-layouts, local_apply(): cell_values = full_list[slot_map]  247 us
    unnamed x12, blocking collectives  178 us
    ppermute x48, starting transfers between devices, shifted(): lax.ppermute(value, axis, [(source, source + steps) for source in range(i...  141 us
    gather x3, local copies, waits for them, and re-layouts, operate(): ghosts = carry_out(vector[send_lists])  69.1 us
    scatter-add x3, other arithmetic, operate(): return result.at[flat_lists].add(returned.reshape(-1))  67.4 us
    unnamed x79, local copies, waits for them, and re-layouts  40.2 us
    scatter-add x3, other arithmetic, local_apply(): spread = summed[:split_at].at[masters.reshape(-1)].add((weights * summed[...  22.5 us
  transfers between devices with their start and end apart: 48, of which 10 were waited for; matrix products, arithmetic and copies ran while one was open for 0% of the time, Pallas kernels for 0%

profile of v1, /device:TPU:1, one launch (start us, length us, event | category | flops | bytes accessed | tf_op | source)
XLA Modules:
  0.0 1085.9 jit_solution(9137621864166917298)
XLA Ops:
  2.1 23.0 %gather_fusion = f32[4096]{0:T(1024)S(1)} fusion(f32[8192]{0:T(1024)S(1)} %copy-done, s32[4096]{0:T(1024)S(1)} %broadcast_clamp_fusion), kind=kCustom, calls=%fused_computation | custom fusion | bytes 49152 | tf_op jit(solution)/shard_map/gather | solution.py:132
  61.1 82.3 %gather_fusion.2 = f32[16000]{0:T(1024)S(1)} fusion(f32[12544]{0:T(1024)S(1)} %pad_maximum_fusion, s32[16384]{0:T(1024)S(1)} %pad_clamp_fusion), kind=kCustom, calls=%fused_computation.2 | custom fusion | bytes 192000 | tf_op jit(solution)/shard_map/gather | solution.py:88
  143.8 85.1 %scatter_custom_fusion = f32[12544]{0:T(1024)S(1)} fusion(s32[16000]{0:T(1024)S(1)} %fusion.7, f32[16000]{0:T(1024)S(1)} %bitcast.143, f32[]{:T(128)} %constant.8.clone.1), kind=kCustom, calls=%fused_computation.59 | custom fusion | flops 16000 | bytes 50180 | tf_op jit(solution)/shard_map/scatter-add | solution.py:91
  229.0 7.4 scatter_fusion
  264.3 22.5 %scatter_fusion.1 = f32[8192]{0:T(1024)S(1)} fusion(f32[8192]{0:T(1024)S(1)} %slice_add_fusion.2, s32[4096]{0:T(1024)S(1)} %bitcast.129, f32[4096]{0:T(1024)S(1)} %bitcast.140), kind=kCustom, calls=%fused_computation.11 | custom fusion | flops 4096 | bytes 65536 | tf_op jit(solution)/shard_map/scatter-add | solution.py:138
  291.6 30.8 %all-reduce.29 = (f32[8]{0:T(128)S(1)}, f32[8]{0:T(128)S(1)}) all-reduce(f32[8]{0:T(128)S(1)} %dynamic-update-slice, f32[8]{0:T(128)S(1)} %dynamic-update-slice.4), channel_id=1, replica_groups=mesh['gx'=8,'gy_0'=4,'gy_1'=8,'gy_2'=2] {'gx'}, use_global_device_ids=true, to_apply=%add | all-reduce | flops 16 | bytes 128
  338.7 13.4 %all-reduce.26 = (f32[8]{0:T(128)S(1)}, f32[8]{0:T(128)S(1)}) all-reduce(f32[8]{0:T(128)S(1)} %dynamic-update-slice.2, f32[8]{0:T(128)S(1)} %dynamic-update-slice.6), channel_id=1, replica_groups=mesh['gx'=8,'gy_0'=4,'gy_1'=8,'gy_2'=2] {'gy_1'}, use_global_device_ids=true, to_apply=%add.2 | all-reduce | flops 16 | bytes 128
  356.1 12.6 %all-reduce.35 = (f32[2]{0:T(128)S(1)}, f32[2]{0:T(128)S(1)}) all-reduce(f32[2]{0:T(128)S(1)} %dynamic-update-slice.3, f32[2]{0:T(128)S(1)} %dynamic-update-slice.7), channel_id=1, replica_groups=mesh['gx'=8,'gy_0'=4,'gy_1'=8,'gy_2'=2] {'gy_2'}, use_global_device_ids=true, to_apply=%add.3 | all-reduce | flops 4 | bytes 32
  371.3 23.0 %gather_fusion.3 = f32[4096]{0:T(1024)S(1)} fusion(f32[8192]{0:T(1024)S(1)} %multiply_subtract_fusion.2, s32[4096]{0:T(1024)S(1)} %broadcast_clamp_fusion), kind=kCustom, calls=%fused_computation.3 | custom fusion | bytes 49152 | tf_op jit(solution)/shard_map/gather | solution.py:132
  423.7 82.3 %gather_fusion.5 = f32[16000]{0:T(1024)S(1)} fusion(f32[12544]{0:T(1024)S(1)} %pad_maximum_fusion.1, s32[16384]{0:T(1024)S(1)} %pad_clamp_fusion), kind=kCustom, calls=%fused_computation.5 | custom fusion | bytes 192000 | tf_op jit(solution)/shard_map/gather | solution.py:88
  506.5 85.1 %scatter_custom_fusion.3 = f32[12544]{0:T(1024)S(1)} fusion(s32[16000]{0:T(1024)S(1)} %fusion.7, f32[16000]{0:T(1024)S(1)} %bitcast.144, f32[]{:T(128)} %constant.8.clone.1), kind=kCustom, calls=%fused_computation.57 | custom fusion | flops 16000 | bytes 50180 | tf_op jit(solution)/shard_map/scatter-add | solution.py:91
  591.7 7.4 scatter_fusion.2
  627.9 22.5 %scatter_fusion.3 = f32[8192]{0:T(1024)S(1)} fusion(f32[8192]{0:T(1024)S(1)} %slice_add_fusion.1, s32[4096]{0:T(1024)S(1)} %bitcast.130, f32[4096]{0:T(1024)S(1)} %bitcast.141), kind=kCustom, calls=%fused_computation.14 | custom fusion | flops 4096 | bytes 65536 | tf_op jit(solution)/shard_map/scatter-add | solution.py:138
  653.8 25.2 %all-reduce.28 = (f32[8]{0:T(128)S(1)}, f32[8]{0:T(128)S(1)}) all-reduce(f32[8]{0:T(128)S(1)} %dynamic-update-slice.8, f32[8]{0:T(128)S(1)} %dynamic-update-slice.12), channel_id=1, replica_groups=mesh['gx'=8,'gy_0'=4,'gy_1'=8,'gy_2'=2] {'gx'}, use_global_device_ids=true, to_apply=%add.8 | all-reduce | flops 16 | bytes 128
  692.8 11.5 %all-reduce.25 = (f32[8]{0:T(128)S(1)}, f32[8]{0:T(128)S(1)}) all-reduce(f32[8]{0:T(128)S(1)} %dynamic-update-slice.10, f32[8]{0:T(128)S(1)} %dynamic-update-slice.14), channel_id=1, replica_groups=mesh['gx'=8,'gy_0'=4,'gy_1'=8,'gy_2'=2] {'gy_1'}, use_global_device_ids=true, to_apply=%add.10 | all-reduce | flops 16 | bytes 128
  708.3 12.9 %all-reduce.34 = (f32[2]{0:T(128)S(1)}, f32[2]{0:T(128)S(1)}) all-reduce(f32[2]{0:T(128)S(1)} %dynamic-update-slice.11, f32[2]{0:T(128)S(1)} %dynamic-update-slice.15), channel_id=1, replica_groups=mesh['gx'=8,'gy_0'=4,'gy_1'=8,'gy_2'=2] {'gy_2'}, use_global_device_ids=true, to_apply=%add.11 | all-reduce | flops 4 | bytes 32
  726.9 23.0 %gather_fusion.6 = f32[4096]{0:T(1024)S(1)} fusion(f32[8192]{0:T(1024)S(1)} %multiply_subtract_fusion.1, s32[4096]{0:T(1024)S(1)} %broadcast_clamp_fusion), kind=kCustom, calls=%fused_computation.6 | custom fusion | bytes 49152 | tf_op jit(solution)/shard_map/gather | solution.py:132
  779.1 82.3 %gather_fusion.8 = f32[16000]{0:T(1024)S(1)} fusion(f32[12544]{0:T(1024)S(1)} %pad_maximum_fusion.2, s32[16384]{0:T(1024)S(1)} %pad_clamp_fusion), kind=kCustom, calls=%fused_computation.8 | custom fusion | bytes 192000 | tf_op jit(solution)/shard_map/gather | solution.py:88
  861.8 85.1 %scatter_custom_fusion.6 = f32[12544]{0:T(1024)S(1)} fusion(s32[16000]{0:T(1024)S(1)} %fusion.7, f32[16000]{0:T(1024)S(1)} %bitcast.142, f32[]{:T(128)} %constant.8.clone.1), kind=kCustom, calls=%fused_computation.55 | custom fusion | flops 16000 | bytes 50180 | tf_op jit(solution)/shard_map/scatter-add | solution.py:91
  947.0 7.6 scatter_fusion.4
  982.6 22.5 %scatter_fusion.5 = f32[8192]{0:T(1024)S(1)} fusion(f32[8192]{0:T(1024)S(1)} %slice_add_fusion, s32[4096]{0:T(1024)S(1)} %bitcast.131, f32[4096]{0:T(1024)S(1)} %bitcast.139), kind=kCustom, calls=%fused_computation.17 | custom fusion | flops 4096 | bytes 65536 | tf_op jit(solution)/shard_map/scatter-add | solution.py:138
  1008.6 29.5 %all-reduce.27 = (f32[8]{0:T(128)S(1)}, f32[8]{0:T(128)S(1)}) all-reduce(f32[8]{0:T(128)S(1)} %dynamic-update-slice.16, f32[8]{0:T(128)S(1)} %dynamic-update-slice.20), channel_id=1, replica_groups=mesh['gx'=8,'gy_0'=4,'gy_1'=8,'gy_2'=2] {'gx'}, use_global_device_ids=true, to_apply=%add.16 | all-reduce | flops 16 | bytes 128
  1051.9 11.4 %all-reduce.24 = (f32[8]{0:T(128)S(1)}, f32[8]{0:T(128)S(1)}) all-reduce(f32[8]{0:T(128)S(1)} %dynamic-update-slice.18, f32[8]{0:T(128)S(1)} %dynamic-update-slice.22), channel_id=1, replica_groups=mesh['gx'=8,'gy_0'=4,'gy_1'=8,'gy_2'=2] {'gy_1'}, use_global_device_ids=true, to_apply=%add.18 | all-reduce | flops 16 | bytes 128
  1067.2 12.9 %all-reduce.33 = (f32[2]{0:T(128)S(1)}, f32[2]{0:T(128)S(1)}) all-reduce(f32[2]{0:T(128)S(1)} %dynamic-update-slice.19, f32[2]{0:T(128)S(1)} %dynamic-update-slice.23), channel_id=1, replica_groups=mesh['gx'=8,'gy_0'=4,'gy_1'=8,'gy_2'=2] {'gy_2'}, use_global_device_ids=true, to_apply=%add.19 | all-reduce | flops 4 | bytes 32
  (267 shorter events, 252.7 us)
Async XLA Ops:
  25.2 16.6 %collective-permute-start.2 = (f32[512]{0:T(512)S(1)}, f32[512]{0:T(512)S(1)}, u32[]{:S(2)}, u32[]{:S(2)}) collective-permute-start(f32[512]{0:T(512)S(1)} %get-tuple-element.79), channel_id=1, source_target_pairs={{0,3},{1,4},{2,5},{3,6},{4,7},{5,8},{6,9},{7,10},{8,11},{9,12},{10... | collective-permute-start | bytes 6152 | tf_op jit(solution)/shard_map/ppermute | solution.py:15
  30.8 12.3 %collective-permute-start.3 = (f32[512]{0:T(512)S(1)}, f32[512]{0:T(512)S(1)}, u32[]{:S(2)}, u32[]{:S(2)}) collective-permute-start(f32[512]{0:T(512)S(1)} %get-tuple-element.78), channel_id=1, source_target_pairs={{0,4},{1,5},{2,6},{3,7},{4,8},{5,9},{6,10},{7,11},{8,12},{9,13},{1... | collective-permute-start | bytes 6152 | tf_op jit(solution)/shard_map/ppermute | solution.py:15
  38.1 14.2 %collective-permute-start.5 = (f32[512]{0:T(512)S(1)}, f32[512]{0:T(512)S(1)}, u32[]{:S(2)}, u32[]{:S(2)}) collective-permute-start(f32[512]{0:T(512)S(1)} %get-tuple-element.76), channel_id=1, source_target_pairs={{2,0},{3,1},{4,2},{5,3},{6,4},{7,5},{8,6},{9,7},{10,8},{11,9},{12,... | collective-permute-start | bytes 6152 | tf_op jit(solution)/shard_map/ppermute | solution.py:15
  39.4 12.9 %collective-permute-start.6 = (f32[512]{0:T(512)S(1)}, f32[512]{0:T(512)S(1)}, u32[]{:S(2)}, u32[]{:S(2)}) collective-permute-start(f32[512]{0:T(512)S(1)} %get-tuple-element.75), channel_id=1, source_target_pairs={{3,0},{4,1},{5,2},{6,3},{7,4},{8,5},{9,6},{10,7},{11,8},{12,9},{13... | collective-permute-start | bytes 6152 | tf_op jit(solution)/shard_map/ppermute | solution.py:15
  238.4 14.5 %collective-permute-start.9 = (f32[512]{0:T(512)S(1)}, f32[512]{0:T(512)S(1)}, u32[]{:S(2)}, u32[]{:S(2)}) collective-permute-start(f32[512]{0:T(512)S(1)} %get-tuple-element.54), channel_id=1, source_target_pairs={{2,0},{3,1},{4,2},{5,3},{6,4},{7,5},{8,6},{9,7},{10,8},{11,9},{12,... | collective-permute-start | bytes 6152 | tf_op jit(solution)/shard_map/ppermute | solution.py:15
  239.7 17.8 %collective-permute-start.10 = (f32[512]{0:T(512)S(1)}, f32[512]{0:T(512)S(1)}, u32[]{:S(2)}, u32[]{:S(2)}) collective-permute-start(f32[512]{0:T(512)S(1)} %get-tuple-element.53), channel_id=1, source_target_pairs={{3,0},{4,1},{5,2},{6,3},{7,4},{8,5},{9,6},{10,7},{11,8},{12,9},{13... | collective-permute-start | bytes 6152 | tf_op jit(solution)/shard_map/ppermute | solution.py:15
  242.3 21.3 %collective-permute-start.11 = (f32[512]{0:T(512)S(1)}, f32[512]{0:T(512)S(1)}, u32[]{:S(2)}, u32[]{:S(2)}) collective-permute-start(f32[512]{0:T(512)S(1)} %get-tuple-element.52), channel_id=1, source_target_pairs={{4,0},{5,1},{6,2},{7,3},{8,4},{9,5},{10,6},{11,7},{12,8},{13,9},{1... | collective-permute-start | bytes 6152 | tf_op jit(solution)/shard_map/ppermute | solution.py:15
  243.6 20.0 %collective-permute-start.12 = (f32[512]{0:T(512)S(1)}, f32[512]{0:T(512)S(1)}, u32[]{:S(2)}, u32[]{:S(2)}) collective-permute-start(f32[512]{0:T(512)S(1)} %get-tuple-element.51), channel_id=1, source_target_pairs={{0,1},{1,2},{2,3},{3,4},{4,5},{5,6},{6,7},{7,8},{8,9},{9,10},{10,1... | collective-permute-start | bytes 6152 | tf_op jit(solution)/shard_map/ppermute | solution.py:15
  247.9 15.7 %collective-permute-start.13 = (f32[512]{0:T(512)S(1)}, f32[512]{0:T(512)S(1)}, u32[]{:S(2)}, u32[]{:S(2)}) collective-permute-start(f32[512]{0:T(512)S(1)} %get-tuple-element.50), channel_id=1, source_target_pairs={{0,2},{1,3},{2,4},{3,5},{4,6},{5,7},{6,8},{7,9},{8,10},{9,11},{10,... | collective-permute-start | bytes 6152 | tf_op jit(solution)/shard_map/ppermute | solution.py:15
  394.4 13.1 %collective-permute-start.16 = (f32[512]{0:T(512)S(1)}, f32[512]{0:T(512)S(1)}, u32[]{:S(2)}, u32[]{:S(2)}) collective-permute-start(f32[512]{0:T(512)S(1)} %get-tuple-element.73), channel_id=1, source_target_pairs={{0,1},{1,2},{2,3},{3,4},{4,5},{5,6},{6,7},{7,8},{8,9},{9,10},{10,1... | collective-permute-start | bytes 6152 | tf_op jit(solution)/shard_map/ppermute | solution.py:15
  396.3 12.5 %collective-permute-start.17 = (f32[512]{0:T(512)S(1)}, f32[512]{0:T(512)S(1)}, u32[]{:S(2)}, u32[]{:S(2)}) collective-permute-start(f32[512]{0:T(512)S(1)} %get-tuple-element.72), channel_id=1, source_target_pairs={{0,2},{1,3},{2,4},{3,5},{4,6},{5,7},{6,8},{7,9},{8,10},{9,11},{10,... | collective-permute-start | bytes 6152 | tf_op jit(solution)/shard_map/ppermute | solution.py:15
  599.1 12.2 %collective-permute-start.24 = (f32[512]{0:T(512)S(1)}, f32[512]{0:T(512)S(1)}, u32[]{:S(2)}, u32[]{:S(2)}) collective-permute-start(f32[512]{0:T(512)S(1)} %get-tuple-element.47), channel_id=1, source_target_pairs={{1,0},{2,1},{3,2},{4,3},{5,4},{6,5},{7,6},{8,7},{9,8},{10,9},{11,1... | collective-permute-start | bytes 6152 | tf_op jit(solution)/shard_map/ppermute | solution.py:15
  602.3 15.1 %collective-permute-start.25 = (f32[512]{0:T(512)S(1)}, f32[512]{0:T(512)S(1)}, u32[]{:S(2)}, u32[]{:S(2)}) collective-permute-start(f32[512]{0:T(512)S(1)} %get-tuple-element.46), channel_id=1, source_target_pairs={{2,0},{3,1},{4,2},{5,3},{6,4},{7,5},{8,6},{9,7},{10,8},{11,9},{12,... | collective-permute-start | bytes 6152 | tf_op jit(solution)/shard_map/ppermute | solution.py:15
  603.6 17.7 %collective-permute-start.26 = (f32[512]{0:T(512)S(1)}, f32[512]{0:T(512)S(1)}, u32[]{:S(2)}, u32[]{:S(2)}) collective-permute-start(f32[512]{0:T(512)S(1)} %get-tuple-element.45), channel_id=1, source_target_pairs={{3,0},{4,1},{5,2},{6,3},{7,4},{8,5},{9,6},{10,7},{11,8},{12,9},{13... | collective-permute-start | bytes 6152 | tf_op jit(solution)/shard_map/ppermute | solution.py:15
  604.9 22.3 %collective-permute-start.27 = (f32[512]{0:T(512)S(1)}, f32[512]{0:T(512)S(1)}, u32[]{:S(2)}, u32[]{:S(2)}) collective-permute-start(f32[512]{0:T(512)S(1)} %get-tuple-element.44), channel_id=1, source_target_pairs={{4,0},{5,1},{6,2},{7,3},{8,4},{9,5},{10,6},{11,7},{12,8},{13,9},{1... | collective-permute-start | bytes 6152 | tf_op jit(solution)/shard_map/ppermute | solution.py:15
  606.2 21.0 %collective-permute-start.28 = (f32[512]{0:T(512)S(1)}, f32[512]{0:T(512)S(1)}, u32[]{:S(2)}, u32[]{:S(2)}) collective-permute-start(f32[512]{0:T(512)S(1)} %get-tuple-element.43), channel_id=1, source_target_pairs={{0,1},{1,2},{2,3},{3,4},{4,5},{5,6},{6,7},{7,8},{8,9},{9,10},{10,1... | collective-permute-start | bytes 6152 | tf_op jit(solution)/shard_map/ppermute | solution.py:15
  611.3 15.8 %collective-permute-start.29 = (f32[512]{0:T(512)S(1)}, f32[512]{0:T(512)S(1)}, u32[]{:S(2)}, u32[]{:S(2)}) collective-permute-start(f32[512]{0:T(512)S(1)} %get-tuple-element.42), channel_id=1, source_target_pairs={{0,2},{1,3},{2,4},{3,5},{4,6},{5,7},{6,8},{7,9},{8,10},{9,11},{10,... | collective-permute-start | bytes 6152 | tf_op jit(solution)/shard_map/ppermute | solution.py:15
  750.0 12.9 %collective-permute-start.32 = (f32[512]{0:T(512)S(1)}, f32[512]{0:T(512)S(1)}, u32[]{:S(2)}, u32[]{:S(2)}) collective-permute-start(f32[512]{0:T(512)S(1)} %get-tuple-element.65), channel_id=1, source_target_pairs={{0,1},{1,2},{2,3},{3,4},{4,5},{5,6},{6,7},{7,8},{8,9},{9,10},{10,1... | collective-permute-start | bytes 6152 | tf_op jit(solution)/shard_map/ppermute | solution.py:15
  752.5 11.7 %collective-permute-start.33 = (f32[512]{0:T(512)S(1)}, f32[512]{0:T(512)S(1)}, u32[]{:S(2)}, u32[]{:S(2)}) collective-permute-start(f32[512]{0:T(512)S(1)} %get-tuple-element.64), channel_id=1, source_target_pairs={{0,2},{1,3},{2,4},{3,5},{4,6},{5,7},{6,8},{7,9},{8,10},{9,11},{10,... | collective-permute-start | bytes 6152 | tf_op jit(solution)/shard_map/ppermute | solution.py:15
  957.8 14.3 %collective-permute-start.41 = (f32[512]{0:T(512)S(1)}, f32[512]{0:T(512)S(1)}, u32[]{:S(2)}, u32[]{:S(2)}) collective-permute-start(f32[512]{0:T(512)S(1)} %get-tuple-element.38), channel_id=1, source_target_pairs={{2,0},{3,1},{4,2},{5,3},{6,4},{7,5},{8,6},{9,7},{10,8},{11,9},{12,... | collective-permute-start | bytes 6152 | tf_op jit(solution)/shard_map/ppermute | solution.py:15
  959.1 16.8 %collective-permute-start.42 = (f32[512]{0:T(512)S(1)}, f32[512]{0:T(512)S(1)}, u32[]{:S(2)}, u32[]{:S(2)}) collective-permute-start(f32[512]{0:T(512)S(1)} %get-tuple-element.37), channel_id=1, source_target_pairs={{3,0},{4,1},{5,2},{6,3},{7,4},{8,5},{9,6},{10,7},{11,8},{12,9},{13... | collective-permute-start | bytes 6152 | tf_op jit(solution)/shard_map/ppermute | solution.py:15
  960.4 21.4 %collective-permute-start.43 = (f32[512]{0:T(512)S(1)}, f32[512]{0:T(512)S(1)}, u32[]{:S(2)}, u32[]{:S(2)}) collective-permute-start(f32[512]{0:T(512)S(1)} %get-tuple-element.36), channel_id=1, source_target_pairs={{4,0},{5,1},{6,2},{7,3},{8,4},{9,5},{10,6},{11,7},{12,8},{13,9},{1... | collective-permute-start | bytes 6152 | tf_op jit(solution)/shard_map/ppermute | solution.py:15
  961.7 20.1 %collective-permute-start.44 = (f32[512]{0:T(512)S(1)}, f32[512]{0:T(512)S(1)}, u32[]{:S(2)}, u32[]{:S(2)}) collective-permute-start(f32[512]{0:T(512)S(1)} %get-tuple-element.35), channel_id=1, source_target_pairs={{0,1},{1,2},{2,3},{3,4},{4,5},{5,6},{6,7},{7,8},{8,9},{9,10},{10,1... | collective-permute-start | bytes 6152 | tf_op jit(solution)/shard_map/ppermute | solution.py:15
  966.0 15.8 %collective-permute-start.45 = (f32[512]{0:T(512)S(1)}, f32[512]{0:T(512)S(1)}, u32[]{:S(2)}, u32[]{:S(2)}) collective-permute-start(f32[512]{0:T(512)S(1)} %get-tuple-element.34), channel_id=1, source_target_pairs={{0,2},{1,3},{2,4},{3,5},{4,6},{5,7},{6,8},{7,9},{8,10},{9,11},{10,... | collective-permute-start | bytes 6152 | tf_op jit(solution)/shard_map/ppermute | solution.py:15
  (33 other events, 378.2 us)
